TPU v7x, 32 devices: a whole 2x2x4 slice. The times are simulated.
32 devices in a mesh: tp: 4 (over x, core), cp: 8 (over z, y).
Axes of the slice: x: 2, y: 2, z: 4, core: 2. Of those that a mesh axis runs over, the one named last changes fastest.
Arguments:
- tokens: bfloat16 [128, 8192], P(('cp', 'tp')), may hold values from -6 to 6
- attention_gain: float32 [8192], replicated, may hold values from 0.1 to 1.9
- query_weight: bfloat16 [8192, 8192], P('cp', 'tp'), may hold values from -0.0625 to 0.0625
- key_weight: bfloat16 [8192, 1024], P('cp', 'tp'), may hold values from -0.0625 to 0.0625
- value_weight: bfloat16 [8192, 1024], P('cp', 'tp'), may hold values from -0.0625 to 0.0625
- out_weight: bfloat16 [8192, 8192], P('tp', 'cp'), may hold values from -0.0625 to 0.0625
- feed_gain: float32 [8192], replicated, may hold values from 0.1 to 1.9
- gate_weight: bfloat16 [8192, 28672], P('tp', 'cp'), may hold values from -0.0625 to 0.0625
- up_weight: bfloat16 [8192, 28672], P('tp', 'cp'), may hold values from -0.0625 to 0.0625
- down_weight: bfloat16 [28672, 8192], P('cp', 'tp'), may hold values from -0.03125 to 0.03125
Outputs:
- attended: bfloat16 [128, 8192], P(('cp', 'tp'))
- mixed: bfloat16 [128, 8192], P(('cp', 'tp'))
All inputs are finite; a program needn't handle non-finite values.
Results may differ from a plain program's by a relative error of at most 0.035.
Values may be sent and summed in bfloat16 or wider, within the bound.
A program may use at most 128 MiB of HBM per device.

v0:
```python
import jax
import jax.numpy as jnp
from jax import lax
from jax.sharding import PartitionSpec as P

HD = 128


epsilon = 1e-05
rope_base = 500000.0
masked = -1e30


def scattered(product, extent, axis):
    everything = product(jnp.int32(0), lax.axis_size(axis) * extent)
    own = lax.psum_scatter(everything.astype(jnp.bfloat16), axis, scatter_dimension=0, tiled=True)
    return own.astype(jnp.float32)


def folded(share, axis, dim, step, start):
    def gathered(part):
        return lax.all_gather(part, axis, axis=dim, tiled=True)

    return step(start, jax.tree.map(gathered, share), jnp.int32(0))


def on_whole(share, axis, dim, apply):
    everything = lax.all_gather(share, axis, axis=dim, tiled=True)
    return apply(everything, jnp.int32(0))


def normalize(values, gain):
    widened = values.astype(jnp.float32)
    mean_square = jnp.mean(widened * widened, axis=-1, keepdims=True)
    return (widened * lax.rsqrt(mean_square + epsilon) * gain).astype(jnp.bfloat16)


def rotate(values, positions):
    row_count = values.shape[0]
    heads = values.reshape(row_count, -1, HD)
    half = HD // 2
    inverse = rope_base ** (-(jnp.arange(half, dtype=jnp.float32) * 2.0 / HD))
    angles = positions.astype(jnp.float32)[:, None] * inverse[None, :]
    cosine = jnp.cos(angles)[:, None, :]
    sine = jnp.sin(angles)[:, None, :]
    first = heads[..., :half]
    second = heads[..., half:]
    turned = jnp.concatenate(
        [first * cosine - second * sine, second * cosine + first * sine], axis=-1
    )
    return turned.reshape(row_count, -1)


def activate(units, unit_width):
    return (jax.nn.silu(units[:, :unit_width]) * units[:, unit_width:]).astype(jnp.bfloat16)


def per_device(
    tokens,
    attention_gain,
    query_weight,
    key_weight,
    value_weight,
    out_weight,
    feed_gain,
    gate_weight,
    up_weight,
    down_weight,
):
    tensor_ways = lax.axis_size("tp")
    local_rows = tokens.shape[0]
    block_rows = local_rows * tensor_ways
    normed = normalize(tokens, attention_gain)
    block_tokens = lax.all_gather(normed, "tp", axis=0, tiled=True)
    columns = lax.all_to_all(block_tokens, "cp", split_axis=1, concat_axis=0, tiled=True)
    query_width = query_weight.shape[1]
    key_width = key_weight.shape[1]

    def project(start, count):
        picked = lax.dynamic_slice_in_dim(columns, start, count, 0)
        return jnp.concatenate(
            [
                jnp.dot(picked, query_weight, preferred_element_type=jnp.float32),
                jnp.dot(picked, key_weight, preferred_element_type=jnp.float32),
                jnp.dot(picked, value_weight, preferred_element_type=jnp.float32),
            ],
            axis=1,
        )

    summed = scattered(project, block_rows, "cp")
    positions = lax.axis_index("cp") * block_rows + jnp.arange(block_rows, dtype=jnp.int32)
    query = rotate(summed[:, :query_width], positions).astype(jnp.bfloat16)
    keys = rotate(summed[:, query_width : query_width + key_width], positions).astype(jnp.bfloat16)
    values = summed[:, query_width + key_width :].astype(jnp.bfloat16)
    shared_heads = key_width // HD
    group_size = query_width // key_width
    query_heads = query.reshape(block_rows, shared_heads, group_size, HD)
    scale = HD ** (-0.5)

    def attend(carry, piece, start):
        running_top, running_total, weighted = carry
        key_piece, value_piece = piece
        piece_rows = key_piece.shape[0]
        key_heads = key_piece.reshape(piece_rows, shared_heads, HD)
        value_heads = value_piece.reshape(piece_rows, shared_heads, HD)
        scores = (
            jnp.einsum("qkgd,skd->kgqs", query_heads, key_heads, preferred_element_type=jnp.float32)
            * scale
        )
        key_positions = start + jnp.arange(piece_rows, dtype=jnp.int32)
        allowed = key_positions[None, :] <= positions[:, None]
        scores = jnp.where(allowed, scores, masked)
        new_top = jnp.maximum(running_top, jnp.max(scores, axis=-1))
        weights = jnp.where(allowed, jnp.exp(scores - new_top[..., None]), 0.0)
        factor = jnp.exp(running_top - new_top)
        new_total = running_total * factor + jnp.sum(weights, axis=-1)
        new_weighted = weighted * factor[..., None] + jnp.einsum(
            "kgqs,skd->kgqd",
            weights,
            value_heads.astype(jnp.float32),
            precision=lax.Precision.HIGHEST,
        )
        return (new_top, new_total, new_weighted)

    head_shape = (shared_heads, group_size, block_rows)
    initial = (
        jnp.full(head_shape, masked, jnp.float32),
        jnp.zeros(head_shape, jnp.float32),
        jnp.zeros(head_shape + (HD,), jnp.float32),
    )
    final_top, final_total, final_weighted = folded((keys, values), "cp", 0, attend, initial)
    attention = (
        (final_weighted / final_total[..., None])
        .transpose(2, 0, 1, 3)
        .reshape(block_rows, query_width)
        .astype(jnp.bfloat16)
    )

    def output_rows(piece, start):
        return jnp.dot(piece, out_weight, preferred_element_type=jnp.float32)

    partial_out = on_whole(attention, "cp", 0, output_rows)
    regrouped = lax.all_to_all(
        partial_out.astype(jnp.bfloat16), "cp", split_axis=0, concat_axis=1, tiled=True
    ).astype(partial_out.dtype)
    projected = lax.psum_scatter(
        regrouped.astype(jnp.bfloat16), "tp", scatter_dimension=0, tiled=True
    ).astype(jnp.float32)
    attended = (tokens.astype(jnp.float32) + projected).astype(jnp.bfloat16)
    normed_feed = normalize(attended, feed_gain)
    spread_rows = lax.all_to_all(normed_feed, "tp", split_axis=1, concat_axis=0, tiled=True)
    unit_width = gate_weight.shape[1]

    def unit_rows(piece, start):
        return jnp.concatenate(
            [
                jnp.dot(piece, gate_weight, preferred_element_type=jnp.float32),
                jnp.dot(piece, up_weight, preferred_element_type=jnp.float32),
            ],
            axis=1,
        )

    partial_units = on_whole(spread_rows, "cp", 0, unit_rows)
    unit_share = lax.psum_scatter(
        partial_units.astype(jnp.bfloat16), "tp", scatter_dimension=0, tiled=True
    ).astype(jnp.float32)
    hidden = lax.all_gather(activate(unit_share, unit_width), "tp", axis=0, tiled=True)

    def down_rows(start, count):
        picked = lax.dynamic_slice_in_dim(hidden, start, count, 0)
        return jnp.dot(picked, down_weight, preferred_element_type=jnp.float32)

    reduced = scattered(down_rows, block_rows, "cp")
    lowered = lax.all_to_all(
        reduced.astype(jnp.bfloat16), "tp", split_axis=0, concat_axis=1, tiled=True
    ).astype(reduced.dtype)
    mixed = (attended.astype(jnp.float32) + lowered).astype(jnp.bfloat16)
    return (attended, mixed)


def solution(mesh):
    in_specs = (
        P(("cp", "tp"), None),
        P(),
        P("cp", "tp"),
        P("cp", "tp"),
        P("cp", "tp"),
        P("tp", "cp"),
        P(),
        P("tp", "cp"),
        P("tp", "cp"),
        P("cp", "tp"),
    )
    out_specs = (P(("cp", "tp"), None), P(("cp", "tp"), None))
    return jax.shard_map(
        per_device, mesh=mesh, in_specs=in_specs, out_specs=out_specs, check_vma=False
    )
```

profile of v0, /device:TPU:0, one launch (start us, length us, event | category | flops | bytes accessed | tf_op | source)
XLA Modules:
  0.0 424.5 jit_solution(17617829598603996720)
XLA Ops:
  7.2 0.0 copy-start
  7.2 0.0 reduce-scatter.4.cloned.1.call-start
  7.2 1.1 fusion.6
  8.3 0.9 fusion.15
  9.3 7.3 %all-gather = bf16[4,4,8192]{2,1,0:T(4,128)(2,1)S(1)} all-gather(bf16[1,4,8192]{2,1,0:T(4,128)(2,1)S(1)} %fusion.15), channel_id=1, replica_groups=mesh['tp'=4,'cp'=8] {'tp'}, dimensions={0}, use_global_device_ids=true | all-gather | bytes 327680 | tf_op jit(solution)/shard_map/all_gather | solution.py:74
  16.5 0.2 all_to_all.52
  16.7 0.2 copy.33
  16.9 15.1 %all_to_all.70 = bf16[16,8,1024]{2,0,1:T(8,128)(2,1)S(1)} all-to-all(bf16[16,8,1024]{2,0,1:T(8,128)(2,1)S(1)} %copy.33), channel_id=1, replica_groups=mesh['tp'=4,'cp'=8] {'cp'}, dimensions={1} | all-to-all | bytes 524288 | tf_op jit(solution)/shard_map/all_to_all | solution.py:75
  31.9 0.0 copy-done
  31.9 0.2 convolution_convert_fusion.5
  32.2 1.3 convolution_convert_fusion.6
  33.5 2.9 convolution_convert_fusion.3
  36.4 0.9 pad_maximum_fusion.1
  37.3 0.0 reduce-scatter.4.cloned.1.call-update
  37.3 0.0 all-reduce.3.cloned.1.call-start
  37.4 0.1 iota_compare_fusion
  37.5 0.1 multiply_cosine_fusion
  37.6 62.3 %reduce-scatter.4.cloned.1.call-done = bf16[16,2560]{1,0:T(8,128)(2,1)} async-done(((bf16[128,2560]{1,0:T(8,128)(2,1)}), bf16[16,2560]{1,0:T(8,128)(2,1)}) %reduce-scatter.4.cloned.1.call-update) | async-done | bytes 81936 | tf_op jit(solution)/shard_map/reduce_scatter | solution.py:16
  99.9 0.7 slice.37
  100.6 0.1 subtract_convert_fusion.1
  100.7 0.1 pad_maximum_fusion.3
  100.8 30.4 %all_gather.19 = bf16[128,256]{1,0:T(8,128)(2,1)S(1)} all-gather(bf16[16,256]{1,0:T(8,128)(2,1)S(1)} %bitcast.84), channel_id=1, replica_groups=mesh['tp'=4,'cp'=8] {'cp'}, dimensions={0}, use_global_device_ids=true | all-gather | bytes 73728 | tf_op jit(solution)/shard_map/all_gather | solution.py:22
  131.2 0.1 copy.34
  131.4 0.7 slice.43
  132.1 30.4 %all_gather.20 = bf16[128,256]{1,0:T(8,128)(2,1)S(1)} all-gather(bf16[16,256]{1,0:T(8,128)(2,1)S(1)} %slice.43), channel_id=1, replica_groups=mesh['tp'=4,'cp'=8] {'cp'}, dimensions={0}, use_global_device_ids=true | all-gather | bytes 73728 | tf_op jit(solution)/shard_map/all_gather | solution.py:22
  162.5 0.9 convert_element_type.80
  163.5 0.1 subtract_convert_fusion
  163.6 0.1 pad_maximum_fusion.2
  163.7 0.0 copy-start.4
  163.7 0.0 copy-start.1
  163.7 0.2 fusion.23
  164.0 0.0 copy-start.3
  164.0 0.2 fusion.14
  164.2 0.3 fusion.4
  164.6 31.7 %all_gather.21 = bf16[128,2048]{1,0:T(8,128)(2,1)S(1)} all-gather(bf16[16,2048]{1,0:T(8,128)(2,1)S(1)} %bitcast.76), channel_id=1, replica_groups=mesh['tp'=4,'cp'=8] {'cp'}, dimensions={0}, use_global_device_ids=true | all-gather | bytes 589824 | tf_op jit(solution)/shard_map/all_gather | solution.py:28
  196.3 2.9 convolution_convert_fusion.4
  199.3 11.2 %all_to_all.71 = bf16[8,16,1024]{2,1,0:T(8,128)(2,1)S(1)} all-to-all(bf16[8,16,1024]{2,1,0:T(8,128)(2,1)S(1)} %bitcast.72), channel_id=1, replica_groups=mesh['tp'=4,'cp'=8] {'cp'}, dimensions={0} | all-to-all | bytes 524288 | tf_op jit(solution)/shard_map/all_to_all | solution.py:143
  210.4 0.7 copy.47
  211.2 0.0 all-reduce.3.cloned.1.call-update
  211.2 0.0 reduce-scatter.6.cloned.1.call-start
  211.2 0.0 copy-done.4
  211.2 0.6 dynamic-slice
  212.5 30.3 %all-reduce.3.cloned.1.call-done = bf16[16,8192]{1,0:T(8,128)(2,1)} async-done(((bf16[16,8192]{1,0:T(8,128)(2,1)}), bf16[16,8192]{1,0:T(8,128)(2,1)}) %all-reduce.3.cloned.1.call-update) | async-done | bytes 262160
  242.8 0.0 copy-done.1
  242.8 1.1 fusion.10
  243.9 0.0 copy-done.3
  243.9 0.1 fusion.12
  244.0 6.5 %all_to_all.72 = bf16[4,4,2048]{2,0,1:T(4,128)(2,1)S(1)} all-to-all(bf16[4,4,2048]{2,0,1:T(4,128)(2,1)S(1)} %bitcast.78), channel_id=1, replica_groups=mesh['tp'=4,'cp'=8] {'tp'}, dimensions={1} | all-to-all | bytes 131072 | tf_op jit(solution)/shard_map/all_to_all | solution.py:151
  250.5 31.5 %all_gather.22 = bf16[128,2048]{1,0:T(8,128)(2,1)S(1)} all-gather(bf16[16,2048]{1,0:T(8,128)(2,1)S(1)} %all_to_all.63), channel_id=1, replica_groups=mesh['tp'=4,'cp'=8] {'cp'}, dimensions={0}, use_global_device_ids=true | all-gather | bytes 589824 | tf_op jit(solution)/shard_map/all_gather | solution.py:28
  282.0 7.3 %convolution_convert_fusion = bf16[128,3584]{1,0:T(8,128)(2,1)S(1)} fusion(bf16[128,2048]{1,0:T(8,128)(2,1)S(1)} %all_gather.22, bf16[2048,3584]{1,0:T(8,128)(2,1)} %param.18), kind=kOutput, calls=%fused_computation | convolution fusion | flops 1879506944 | bytes 16121856 | tf_op jit(solution)/shard_map/dot_general | solution.py:158
  289.3 7.3 %convolution_convert_fusion.1 = bf16[128,3584]{1,0:T(8,128)(2,1)S(1)} fusion(bf16[128,2048]{1,0:T(8,128)(2,1)S(1)} %all_gather.22, bf16[2048,3584]{1,0:T(8,128)(2,1)} %param.17), kind=kOutput, calls=%fused_computation.1 | convolution fusion | flops 1879506944 | bytes 16121856 | tf_op jit(solution)/shard_map/dot_general | solution.py:157
  296.6 1.4 pad_maximum_fusion
  298.0 0.0 reduce-scatter.6.cloned.1.call-update
  298.0 0.0 reduce-scatter.8.cloned.1.call-start
  298.1 29.6 %reduce-scatter.6.cloned.1.call-done = bf16[32,7168]{1,0:T(8,128)(2,1)} async-done(((bf16[128,7168]{1,0:T(8,128)(2,1)}), bf16[32,7168]{1,0:T(8,128)(2,1)}) %reduce-scatter.6.cloned.1.call-update) | async-done | bytes 458768 | tf_op jit(solution)/shard_map/reduce_scatter | solution.py:164
  327.7 1.1 convert_element_type.91
  328.8 0.1 fusion.5
  328.9 8.7 %all_gather.23 = bf16[128,3584]{1,0:T(8,128)(2,1)S(1)} all-gather(bf16[32,3584]{1,0:T(8,128)(2,1)S(1)} %fusion.5), channel_id=1, replica_groups=mesh['tp'=4,'cp'=8] {'tp'}, dimensions={0}, use_global_device_ids=true | all-gather | bytes 1146880 | tf_op jit(solution)/shard_map/all_gather | solution.py:167
  337.6 8.3 %convolution_convert_fusion.2 = bf16[128,2048]{1,0:T(8,128)(2,1)} fusion(bf16[128,3584]{1,0:T(8,128)(2,1)S(1)} %all_gather.23, bf16[3584,2048]{1,0:T(8,128)(2,1)} %param.19), kind=kOutput, calls=%fused_computation.2 | convolution fusion | flops 1879310336 | bytes 16121856 | tf_op jit(solution)/shard_map/dot_general | solution.py:171
  345.9 0.0 reduce-scatter.8.cloned.1.call-update
  345.9 63.8 %reduce-scatter.8.cloned.1.call-done = bf16[16,2048]{1,0:T(8,128)(2,1)} async-done(((bf16[128,2048]{1,0:T(8,128)(2,1)}), bf16[16,2048]{1,0:T(8,128)(2,1)}) %reduce-scatter.8.cloned.1.call-update) | async-done | bytes 65552 | tf_op jit(solution)/shard_map/reduce_scatter | solution.py:16
  409.7 0.9 all_to_all.64
  410.6 6.6 %all_to_all.73 = bf16[4,4,2048]{2,1,0:T(4,128)(2,1)S(1)} all-to-all(bf16[4,4,2048]{2,1,0:T(4,128)(2,1)S(1)} %all_to_all.64), channel_id=1, replica_groups=mesh['tp'=4,'cp'=8] {'tp'}, dimensions={0} | all-to-all | bytes 131072 | tf_op jit(solution)/shard_map/all_to_all | solution.py:174
  417.3 0.7 fusion.13
  (19 shorter events, 0.2 us)
Async XLA Ops:
  7.2 24.8 %copy-start = (bf16[1024,256]{1,0:T(8,128)(2,1)S(1)}, bf16[1024,256]{1,0:T(8,128)(2,1)}, u32[]{:S(2)}) copy-start(bf16[1024,256]{1,0:T(8,128)(2,1)} %param.14) | copy-start | bytes 1572868
  7.2 92.7 %reduce-scatter.4.cloned.1.call-start = ((), (), s32[]{:S(2)}) async-start(), calls=%async_computation.7 | async-start | bytes 737280 | tf_op jit(solution)/shard_map/reduce_scatter | solution.py:16
  37.3 205.5 %all-reduce.3.cloned.1.call-start = ((), (), s32[]{:S(2)}) async-start(), calls=%async_computation.10 | async-start | bytes 524288
  163.7 47.5 %copy-start.4 = (u32[32]{0:T(128)S(1)}, u32[32]{0:T(128)}, u32[]{:S(2)}) copy-start(u32[32]{0:T(128)} %constant.36) | copy-start | bytes 388
  163.7 79.1 %copy-start.1 = (bf16[4,8192]{1,0:T(4,128)(2,1)S(1)}, bf16[4,8192]{1,0:T(4,128)(2,1)}, u32[]{:S(2)}) copy-start(bf16[4,8192]{1,0:T(4,128)(2,1)} %param.10) | copy-start | bytes 196612
  164.0 79.9 %copy-start.3 = (f32[8192]{0:T(1024)S(1)}, f32[8192]{0:T(1024)}, u32[]{:S(2)}) copy-start(f32[8192]{0:T(1024)} %param.16) | copy-start | bytes 98308
  211.2 116.5 %reduce-scatter.6.cloned.1.call-start = ((), (), s32[]{:S(2)}) async-start(), calls=%async_computation.8 | async-start | bytes 2293760 | tf_op jit(solution)/shard_map/reduce_scatter | solution.py:164
  243.9 173.4 %copy-start.2 = (bf16[4,8192]{1,0:T(4,128)(2,1)}, bf16[4,8192]{1,0:T(4,128)(2,1)S(1)}, u32[]{:S(2)}) copy-start(bf16[4,8192]{1,0:T(4,128)(2,1)S(1)} %get-tuple-element.3) | copy-start | bytes 196612
  298.0 111.7 %reduce-scatter.8.cloned.1.call-start = ((), (), s32[]{:S(2)}) async-start(), calls=%async_computation.9 | async-start | bytes 589824 | tf_op jit(solution)/shard_map/reduce_scatter | solution.py:16
Sparse Core Ops, SparseCore 0:
  37.4 62.3 reduce-scatter.3
  211.3 31.4 all-reduce.2
  298.1 29.5 reduce-scatter.5
  346.0 63.6 reduce-scatter.7
where the time goes:
time: 425 us; the launch traced here: 424 us
  waiting for transfers between devices  186 us (44%)
  blocking collectives  179 us (42%)
  matrix products  30.8 us (7%)
  between operations  14.7 us (3%)
  other arithmetic  9.14 us (2%)
    reduce_scatter x2, waiting for transfers between devices, scattered(): lax.psum_scatter(everything.astype(jnp.bfloat16), axis, scatter_dimension...  126 us
    all_gather x2, blocking collectives, on_whole(): everything = lax.all_gather(share, axis, axis=dim, tiled=True)  63.2 us
    all_gather x2, blocking collectives, gathered(): return lax.all_gather(part, axis, axis=dim, tiled=True)  60.9 us
    unnamed x5, waiting for transfers between devices  30.4 us
    reduce_scatter x1, waiting for transfers between devices, per_device(): lax.psum_scatter(partial_units.astype(jnp.bfloat16), 'tp', scatter_dimens...  29.6 us
    all_to_all x1, blocking collectives, per_device(): lax.all_to_all(block_tokens, 'cp', split_axis=1, concat_axis=0, tiled=True)  15.1 us
    all_to_all x1, blocking collectives, per_device(): lax.all_to_all(partial_out.astype(jnp.bfloat16), 'cp', split_axis=0, conc...  11.2 us
    all_gather x1, blocking collectives, per_device(): lax.all_gather(activate(unit_share, unit_width), 'tp', axis=0, tiled=True)  8.65 us
  transfers between devices with their start and end apart: 4, of which 4 were waited for; matrix products, arithmetic and copies ran while one was open for 0% of the time, Pallas kernels for 0%

commit v1 on v0

v1 whole, which is shorter than its diff:
```python
import functools

import jax
import jax.numpy as jnp
import numpy as np
from jax import lax
from jax.experimental import pallas as pl
from jax.experimental.pallas import tpu as pltpu
from jax.sharding import PartitionSpec as P

HD = 128
epsilon = 1e-05
rope_base = 500000.0
masked = -1e30
bf16 = jnp.bfloat16
f32 = jnp.float32
MESH = pl.DeviceIdType.MESH


def tile_of(width, most=512):
    for size in (512, 256, 128):
        if size <= most and width % size == 0:
            return size
    return width


def normalize(values, gain):
    mean_square = jnp.mean(values * values, axis=-1, keepdims=True)
    return (values * lax.rsqrt(mean_square + epsilon) * gain).astype(bf16)


def kernel(
    T,
    C,
    tokens,
    again,
    fgain,
    cosine,
    sine,
    wq_h,
    wk_h,
    wv_h,
    wo_h,
    wg_h,
    wu_h,
    wd_h,
    attended_ref,
    mixed_ref,
    wq,
    wk,
    wv,
    wo,
    wg,
    wu,
    wd,
    xsend,
    xrecv,
    xb,
    stage,
    psend,
    precv,
    kvbuf,
    abuf,
    osend,
    orecv,
    nsend,
    nrecv,
    gu,
    g1recv,
    g2send,
    g2recv,
    hid,
    dsend,
    drecv,
    wsem,
    lsem,
    ssem,
    rsem,
):
    G = C * T
    X = T // 2
    R = tokens.shape[0]
    B = R * T
    N = R * G
    c_me = lax.axis_index("cp")
    t_me = lax.axis_index("tp")
    g_me = c_me * T + t_me
    x_me = lax.div(t_me, 2)
    core = lax.rem(t_me, 2)
    QW = wq.shape[1]
    KW = wk.shape[1]
    DC = wq.shape[0]
    DT = wg.shape[0]
    FW = wg.shape[1]

    weights = [(wq_h, wq), (wk_h, wk), (wv_h, wv), (wo_h, wo), (wg_h, wg), (wu_h, wu), (wd_h, wd)]
    loads = [pltpu.make_async_copy(s, d, wsem.at[i]) for i, (s, d) in enumerate(weights)]

    barrier = pltpu.get_barrier_semaphore()

    @pl.loop(1, G)
    def _(k):
        g = lax.rem(g_me + k, G)
        pl.semaphore_signal(
            barrier, inc=1, device_id={"cp": lax.div(g, T), "tp": lax.rem(g, T)}, device_id_type=MESH
        )

    for load in loads:
        load.start()

    normed = normalize(tokens[...].astype(f32), again[...])
    for c in range(C):
        xsend[c] = normed[:, c * DC : (c + 1) * DC]
    pl.semaphore_wait(barrier, G - 1)

    def remote(src, dst, phase, cp, tp):
        return pltpu.make_async_remote_copy(
            src_ref=src,
            dst_ref=dst,
            send_sem=ssem.at[phase],
            recv_sem=rsem.at[phase],
            device_id={"cp": cp, "tp": tp},
            device_id_type=MESH,
        )

    def to_all(source, buffer, phase):
        own = pltpu.make_async_copy(source(c_me, t_me, g_me), buffer.at[g_me], lsem.at[phase])
        own.start()

        @pl.loop(1, G)
        def _(k):
            g = lax.rem(g_me + k, G)
            c = lax.div(g, T)
            t = lax.rem(g, T)
            remote(source(c, t, g), buffer.at[g_me], phase, c, t).start()

        return own

    def to_cp(source, buffer, phase):
        @pl.loop(1, C)
        def _(k):
            c = lax.rem(c_me + k, C)
            remote(source(c), buffer.at[c_me], phase, c, t_me).start()

    def bytes_wait(view, sem):
        pltpu.make_async_copy(view, view, sem).wait()

    own = to_all(lambda c, t, g: xsend.at[c], xrecv, 0)
    own.wait()
    bytes_wait(xrecv.at[pl.ds(0, G - 1)], rsem.at[0])
    for g in range(G):
        stage[g * R : (g + 1) * R, :DC] = xrecv[g].astype(f32)
    xb[:, :DC] = stage[:, :DC].astype(bf16)

    def project(weight, width, base):
        size = tile_of(width)

        @pl.loop(0, width // size)
        def _(n):
            at = pl.multiple_of(n * size, size)
            part = jnp.dot(xb[:, :DC], weight[:, pl.ds(at, size)], preferred_element_type=f32)
            psend[:, :, pl.ds(pl.multiple_of(base + at, 128), size)] = part.reshape(C, B, size).astype(bf16)

    loads[0].wait()
    project(wq, QW, 0)
    loads[1].wait()
    project(wk, KW, QW)
    loads[2].wait()
    project(wv, KW, QW + KW)
    to_cp(lambda c: psend.at[c], precv, 1)
    bytes_wait(precv.at[pl.ds(0, C - 1)], rsem.at[1])

    row0 = pl.multiple_of(c_me * B, B)
    cos = cosine[pl.ds(row0, B), :]
    sin = sine[pl.ds(row0, B), :]

    def summed(at, width):
        total = psend[c_me, :, at : at + width].astype(f32)
        for k in range(1, C):
            total += precv[lax.rem(c_me + k, C), :, at : at + width].astype(f32)
        return total

    def turned(head):
        return (head * cos + pltpu.roll(head, HD // 2, 1) * sin).astype(bf16)

    heads = QW // HD
    shared = KW // HD
    group = heads // shared
    for h in range(shared):
        kvbuf[c_me, :, h * HD : (h + 1) * HD] = turned(summed(QW + h * HD, HD))
    kvbuf[c_me, :, KW:] = summed(QW + KW, KW).astype(bf16)
    to_cp(lambda c: kvbuf.at[c_me], kvbuf, 2)
    queries = [turned(summed(h * HD, HD)) for h in range(heads)]
    bytes_wait(kvbuf.at[pl.ds(0, C - 1)], rsem.at[2])

    scale = HD ** (-0.5)
    for s in range(shared):
        q = jnp.concatenate(queries[s * group : (s + 1) * group], axis=0)
        keys = kvbuf[:, :, s * HD : (s + 1) * HD].reshape(N, HD)
        vals = kvbuf[:, :, KW + s * HD : KW + (s + 1) * HD].reshape(N, HD)
        scores = (
            lax.dot_general(q, keys, (((1,), (1,)), ((), ())), preferred_element_type=f32) * scale
        )
        rows = lax.broadcasted_iota(jnp.int32, (group * B, N), 0)
        cols = lax.broadcasted_iota(jnp.int32, (group * B, N), 1)
        allowed = cols <= (rows & (B - 1)) + row0
        scores = jnp.where(allowed, scores, masked)
        top = jnp.max(scores, axis=-1, keepdims=True)
        soft = jnp.where(allowed, jnp.exp(scores - top), 0.0)
        total = jnp.sum(soft, axis=-1, keepdims=True)
        mix = jnp.dot(soft.astype(bf16), vals, preferred_element_type=f32) / total
        for j in range(group):
            h = s * group + j
            abuf[c_me, :, h * HD : (h + 1) * HD] = mix[j * B : (j + 1) * B].astype(bf16)
    to_cp(lambda c: abuf.at[c_me], abuf, 3)
    loads[3].wait()
    bytes_wait(abuf.at[pl.ds(0, C - 1)], rsem.at[3])

    OC = wo.shape[1]
    osize = tile_of(OC)

    @pl.loop(0, OC // osize)
    def _(n):
        at = pl.multiple_of(n * osize, osize)
        stage[:, pl.ds(at, osize)] = jnp.dot(
            abuf[...].reshape(N, QW), wo[:, pl.ds(at, osize)], preferred_element_type=f32
        )

    for g in range(G):
        osend[g] = stage[g * R : (g + 1) * R, :OC].astype(bf16)
    own = to_all(lambda c, t, g: osend.at[g], orecv, 4)
    own.wait()
    bytes_wait(orecv.at[pl.ds(0, G - 1)], rsem.at[4])
    for c in range(C):
        total = tokens[:, c * OC : (c + 1) * OC].astype(f32)
        add = orecv[c * T].astype(f32)
        for t in range(1, T):
            add += orecv[c * T + t].astype(f32)
        attended_ref[:, c * OC : (c + 1) * OC] = (total + add).astype(bf16)

    normed_feed = normalize(attended_ref[...].astype(f32), fgain[...])
    for t in range(T):
        nsend[t] = normed_feed[:, t * DT : (t + 1) * DT]
    own = to_all(lambda c, t, g: nsend.at[t], nrecv, 5)
    loads[4].wait()
    loads[5].wait()
    own.wait()
    bytes_wait(nrecv.at[pl.ds(0, G - 1)], rsem.at[5])
    for g in range(G):
        stage[g * R : (g + 1) * R, :DT] = nrecv[g].astype(f32)
    xb[:, :DT] = stage[:, :DT].astype(bf16)

    fsize = tile_of(FW)
    share = N // T

    @pl.loop(0, FW // fsize)
    def _(n):
        at = pl.multiple_of(n * fsize, fsize)
        for weight, base in ((wg, 0), (wu, FW)):
            part = jnp.dot(xb[:, :DT], weight[:, pl.ds(at, fsize)], preferred_element_type=f32)
            gu[:, :, pl.ds(pl.multiple_of(base + at, 128), fsize)] = part.reshape(T, share, fsize).astype(bf16)

    @pl.loop(0, X)
    def _(x):
        remote(gu.at[2 * x + 1 - core], g1recv.at[x], 6, c_me, 2 * x_me + 1 - core).start()

    bytes_wait(g1recv, rsem.at[6])
    tiles = 2 * FW // fsize
    for k in range(1, X):
        x = lax.rem(x_me + k, X)

        @pl.loop(0, tiles)
        def _(n):
            cols = pl.ds(pl.multiple_of(n * fsize, fsize), fsize)
            g2send[k - 1, :, cols] = (
                gu[2 * x + core, :, cols].astype(f32) + g1recv[x, :, cols].astype(f32)
            ).astype(bf16)

        remote(g2send.at[k - 1], g2recv.at[k - 1], 7, c_me, 2 * x + core).start()
    if X > 1:
        bytes_wait(g2recv, rsem.at[7])

    def unit(cols):
        total = gu[t_me, :, cols].astype(f32) + g1recv[x_me, :, cols].astype(f32)
        for k in range(1, X):
            total += g2recv[k - 1, :, cols].astype(f32)
        return total

    @pl.loop(0, FW // fsize)
    def _(n):
        at = pl.multiple_of(n * fsize, fsize)
        gate = unit(pl.ds(at, fsize))
        up = unit(pl.ds(pl.multiple_of(FW + at, 128), fsize))
        hid[t_me, :, pl.ds(at, fsize)] = (gate / (1.0 + jnp.exp(-gate)) * up).astype(bf16)

    partner = 2 * x_me + 1 - core
    for k in range(1, X):
        remote(hid.at[t_me], hid.at[t_me], 8, c_me, 2 * lax.rem(x_me + k, X) + core).start()
    remote(hid.at[t_me], hid.at[t_me], 9, c_me, partner).start()
    if X > 1:
        bytes_wait(hid.at[pl.ds(0, X - 1)], rsem.at[8])
        for k in range(1, X):
            t = 2 * lax.rem(x_me + k, X) + core
            remote(hid.at[t], hid.at[t], 9, c_me, partner).start()
    loads[6].wait()
    bytes_wait(hid.at[pl.ds(0, X)], rsem.at[9])

    DW = wd.shape[1]
    dsize = tile_of(DW, 256)

    @pl.loop(0, DW // dsize)
    def _(n):
        at = pl.multiple_of(n * dsize, dsize)
        stage[:, pl.ds(at, dsize)] = jnp.dot(
            hid[...].reshape(N, FW), wd[:, pl.ds(at, dsize)], preferred_element_type=f32
        )

    for g in range(G):
        dsend[g] = stage[g * R : (g + 1) * R, :DW].astype(bf16)
    own = to_all(lambda c, t, g: dsend.at[g], drecv, 10)
    own.wait()
    bytes_wait(drecv.at[pl.ds(0, G - 1)], rsem.at[10])
    for t in range(T):
        add = drecv[t].astype(f32)
        for c in range(1, C):
            add += drecv[c * T + t].astype(f32)
        cols = slice(t * DW, (t + 1) * DW)
        mixed_ref[:, cols] = (attended_ref[:, cols].astype(f32) + add).astype(bf16)

    bytes_wait(xrecv.at[pl.ds(0, G - 1)], ssem.at[0])
    bytes_wait(precv.at[pl.ds(0, C - 1)], ssem.at[1])
    bytes_wait(kvbuf.at[pl.ds(0, C - 1)], ssem.at[2])
    bytes_wait(abuf.at[pl.ds(0, C - 1)], ssem.at[3])
    bytes_wait(orecv.at[pl.ds(0, G - 1)], ssem.at[4])
    bytes_wait(nrecv.at[pl.ds(0, G - 1)], ssem.at[5])
    bytes_wait(g1recv, ssem.at[6])
    if X > 1:
        bytes_wait(g2recv, ssem.at[7])
        bytes_wait(hid.at[pl.ds(0, X - 1)], ssem.at[8])
    bytes_wait(hid.at[pl.ds(0, X)], ssem.at[9])
    bytes_wait(drecv.at[pl.ds(0, G - 1)], ssem.at[10])


def tables(count):
    half = HD // 2
    inverse = rope_base ** (-(np.arange(half, dtype=np.float64) * 2.0 / HD))
    angles = np.arange(count, dtype=np.float64)[:, None] * inverse[None, :]
    cos = np.concatenate([np.cos(angles), np.cos(angles)], axis=1)
    sin = np.concatenate([-np.sin(angles), np.sin(angles)], axis=1)
    return jnp.asarray(cos, f32), jnp.asarray(sin, f32)


def per_device(tokens, again, wq, wk, wv, wo, fgain, wg, wu, wd, *, T, C):
    R, D = tokens.shape
    G = T * C
    X = T // 2
    N = R * G
    B = R * T
    QW, KW, FW = wq.shape[1], wk.shape[1], wg.shape[1]
    DC, DT, OC, DW = wq.shape[0], wg.shape[0], wo.shape[1], wd.shape[1]
    cos, sin = tables(N)
    vm = pl.BlockSpec(memory_space=pltpu.VMEM)
    hbm = pl.BlockSpec(memory_space=pl.ANY)
    wide = max(DC, DT, OC, DW)

    def buf(*shape, dtype=bf16):
        return pltpu.VMEM(shape, dtype)

    macs = N * sum(w.size for w in (wq, wk, wv, wo, wg, wu, wd))
    return pl.pallas_call(
        functools.partial(kernel, T, C),
        out_shape=(jax.ShapeDtypeStruct((R, D), bf16), jax.ShapeDtypeStruct((R, D), bf16)),
        in_specs=[vm] * 5 + [hbm] * 7,
        out_specs=(vm, vm),
        scratch_shapes=[
            *[buf(*w.shape) for w in (wq, wk, wv, wo, wg, wu, wd)],
            buf(C, R, DC),
            buf(G, R, DC),
            buf(N, max(DC, DT)),
            buf(N, wide, dtype=f32),
            buf(C, B, QW + 2 * KW),
            buf(C, B, QW + 2 * KW),
            buf(C, B, 2 * KW),
            buf(C, B, QW),
            buf(G, R, OC),
            buf(G, R, OC),
            buf(T, R, DT),
            buf(G, R, DT),
            buf(T, N // T, 2 * FW),
            buf(X, N // T, 2 * FW),
            buf(max(X - 1, 1), N // T, 2 * FW),
            buf(max(X - 1, 1), N // T, 2 * FW),
            buf(T, N // T, FW),
            buf(G, R, DW),
            buf(G, R, DW),
            pltpu.SemaphoreType.DMA((7,)),
            pltpu.SemaphoreType.DMA((11,)),
            pltpu.SemaphoreType.DMA((11,)),
            pltpu.SemaphoreType.DMA((11,)),
        ],
        compiler_params=pltpu.CompilerParams(
            collective_id=0, has_side_effects=True, vmem_limit_bytes=67043328
        ),
        cost_estimate=pl.CostEstimate(flops=2 * macs, bytes_accessed=2 * macs // N, transcendentals=0),
    )(tokens, again.reshape(1, D), fgain.reshape(1, D), cos, sin, wq, wk, wv, wo, wg, wu, wd)


def solution(mesh):
    in_specs = (
        P(("cp", "tp"), None),
        P(),
        P("cp", "tp"),
        P("cp", "tp"),
        P("cp", "tp"),
        P("tp", "cp"),
        P(),
        P("tp", "cp"),
        P("tp", "cp"),
        P("cp", "tp"),
    )
    out_specs = (P(("cp", "tp"), None), P(("cp", "tp"), None))
    body = functools.partial(per_device, T=mesh.shape["tp"], C=mesh.shape["cp"])
    return jax.shard_map(body, mesh=mesh, in_specs=in_specs, out_specs=out_specs, check_vma=False)
```

time: 425 us -> 123 us (0.29)
  the two profiles are of different devices: /device:TPU:0 before, /device:TPU:21 now
where the time goes in v1:
time: 123 us
  Pallas kernels  119 us (97%)
  local copies, waits for them, and re-layouts  2.98 us (2%)
    pallas_call x1, Pallas kernels, per_device(): pl.pallas_call(functools.partial(kernel, T, C), out_shape=(jax.ShapeDtype...  119 us
    unnamed x2, local copies, waits for them, and re-layouts  2.98 us

profile of v1, /device:TPU:21, one launch (start us, length us, event | category | flops | bytes accessed | tf_op | source)
XLA Modules:
  0.0 122.8 jit_solution(11613750443991684298)
XLA Ops:
  0.6 119.2 %shard_map.131 = (bf16[4,8192]{1,0:T(4,128)(2,1)}, bf16[4,8192]{1,0:T(4,128)(2,1)}) custom-call(bf16[4,8192]{1,0:T(4,128)(2,1)} %tokens.1, f32[1,8192]{1,0:T(1,128)} %bitcast.2, f32[1,8192]{1,0:T(1,128)} %bitcast.3, f32[128,128]{1,0:T(8,128)} %constant.4.clone.cosine, f32[128,128]{1,0:T(8,128)} %constant.5.clone.sine, bf16[1024,2048]{1,0:T(8,128)(2,1)} %wq_h.1, ...), custom_call_target="tpu_custom_call" | custom-call | flops 6845104128 | bytes 53477376 | tf_op jit(solution)/shard_map/pallas_call | solution.py:370
  119.8 1.5 %copy.16 = bf16[4,8192]{1,0:T(4,128)(2,1)} copy(bf16[4,8192]{1,0:T(4,128)(2,1)} %get-tuple-element.4) | data formatting | bytes 131072
  121.3 1.5 %copy.17 = bf16[4,8192]{1,0:T(4,128)(2,1)} copy(bf16[4,8192]{1,0:T(4,128)(2,1)} %get-tuple-element.5) | data formatting | bytes 131072

commit v2 on v1

--- a/solution.py
+++ b/solution.py
@@ -76,6 +76,11 @@
     lsem,
     ssem,
     rsem,
+    asem,
+    bsem,
+    r1sem,
+    r2sem,
+    r8sem,
 ):
     G = C * T
     X = T // 2
@@ -113,12 +118,12 @@
         xsend[c] = normed[:, c * DC : (c + 1) * DC]
     pl.semaphore_wait(barrier, G - 1)
 
-    def remote(src, dst, phase, cp, tp):
+    def remote(src, dst, phase, cp, tp, arrival=None):
         return pltpu.make_async_remote_copy(
             src_ref=src,
             dst_ref=dst,
             send_sem=ssem.at[phase],
-            recv_sem=rsem.at[phase],
+            recv_sem=rsem.at[phase] if arrival is None else arrival,
             device_id={"cp": cp, "tp": tp},
             device_id_type=MESH,
         )
@@ -145,6 +150,25 @@
     def bytes_wait(view, sem):
         pltpu.make_async_copy(view, view, sem).wait()
 
+    def cp_gather(buffer, phase, sems):
+        pair = c_me + 1 - 2 * lax.rem(c_me, 2)
+        half = C // 2
+        own = buffer.at[c_me]
+
+        @pl.loop(1, half)
+        def _(k):
+            remote(own, own, phase, lax.rem(c_me + 2 * k, C), t_me, sems.at[k]).start()
+
+        remote(own, own, phase, pair, t_me).start()
+
+        @pl.loop(1, half)
+        def _(k):
+            came = buffer.at[lax.rem(c_me + C - 2 * k, C)]
+            bytes_wait(came, sems.at[k])
+            remote(came, came, phase, pair, t_me).start()
+
+        bytes_wait(buffer.at[pl.ds(0, half)], rsem.at[phase])
+
     own = to_all(lambda c, t, g: xsend.at[c], xrecv, 0)
     own.wait()
     bytes_wait(xrecv.at[pl.ds(0, G - 1)], rsem.at[0])
@@ -159,7 +183,13 @@
         def _(n):
             at = pl.multiple_of(n * size, size)
             part = jnp.dot(xb[:, :DC], weight[:, pl.ds(at, size)], preferred_element_type=f32)
-            psend[:, :, pl.ds(pl.multiple_of(base + at, 128), size)] = part.reshape(C, B, size).astype(bf16)
+            cols = pl.ds(pl.multiple_of(base + at, 128), size)
+            psend[:, :, cols] = part.reshape(C, B, size).astype(bf16)
+
+            @pl.loop(1, C)
+            def _(k):
+                c = lax.rem(c_me + k, C)
+                remote(psend.at[c, :, cols], precv.at[c_me, :, cols], 1, c, t_me).start()
 
     loads[0].wait()
     project(wq, QW, 0)
@@ -167,7 +197,6 @@
     project(wk, KW, QW)
     loads[2].wait()
     project(wv, KW, QW + KW)
-    to_cp(lambda c: psend.at[c], precv, 1)
     bytes_wait(precv.at[pl.ds(0, C - 1)], rsem.at[1])
 
     row0 = pl.multiple_of(c_me * B, B)
@@ -212,9 +241,8 @@
         for j in range(group):
             h = s * group + j
             abuf[c_me, :, h * HD : (h + 1) * HD] = mix[j * B : (j + 1) * B].astype(bf16)
-    to_cp(lambda c: abuf.at[c_me], abuf, 3)
+    cp_gather(abuf, 3, asem)
     loads[3].wait()
-    bytes_wait(abuf.at[pl.ds(0, C - 1)], rsem.at[3])
 
     OC = wo.shape[1]
     osize = tile_of(OC)
@@ -241,44 +269,72 @@
     normed_feed = normalize(attended_ref[...].astype(f32), fgain[...])
     for t in range(T):
         nsend[t] = normed_feed[:, t * DT : (t + 1) * DT]
-    own = to_all(lambda c, t, g: nsend.at[t], nrecv, 5)
+    own = pltpu.make_async_copy(nsend.at[t_me], nrecv.at[c_me, t_me], lsem.at[5])
+    own.start()
+    for k in range(1, T):
+        t = lax.rem(t_me + k, T)
+        remote(nsend.at[t], nrecv.at[c_me, t_me], 5, c_me, t).start()
+    own.wait()
+    bytes_wait(nrecv.at[0, pl.ds(0, T - 1)], rsem.at[5])
+    cp_gather(nrecv, 11, bsem)
     loads[4].wait()
     loads[5].wait()
-    own.wait()
-    bytes_wait(nrecv.at[pl.ds(0, G - 1)], rsem.at[5])
     for g in range(G):
-        stage[g * R : (g + 1) * R, :DT] = nrecv[g].astype(f32)
+        stage[g * R : (g + 1) * R, :DT] = nrecv[g // T, g % T].astype(f32)
     xb[:, :DT] = stage[:, :DT].astype(bf16)
 
     fsize = tile_of(FW)
     share = N // T
 
-    @pl.loop(0, FW // fsize)
+    tiles = FW // fsize
+    partner = 2 * x_me + 1 - core
+
+    def spans(n):
+        at = n * fsize
+        return [pl.ds(pl.multiple_of(base + at, 128), fsize) for base in (0, FW)]
+
+    def compute(n):
+        at = pl.multiple_of(n * fsize, 128)
+        for weight, cols in zip((wg, wu), spans(n)):
+            part = jnp.dot(xb[:, :DT], weight[:, pl.ds(at, fsize)], preferred_element_type=f32)
+            gu[:, :, cols] = part.reshape(T, share, fsize).astype(bf16)
+        for cols in spans(n):
+            for x in range(X):
+                remote(
+                    gu.at[2 * x + 1 - core, :, cols],
+                    g1recv.at[x, :, cols],
+                    6,
+                    c_me,
+                    partner,
+                    r1sem.at[n],
+                ).start()
+
+    def across(n):
+        bytes_wait(g1recv.at[:, :, pl.ds(0, 2 * fsize)], r1sem.at[n])
+        for k in range(1, X):
+            x = lax.rem(x_me + k, X)
+            for cols in spans(n):
+                both = gu[2 * x + core, :, cols].astype(f32) + g1recv[x, :, cols].astype(f32)
+                g2send[k - 1, :, cols] = both.astype(bf16)
+            for cols in spans(n):
+                remote(
+                    g2send.at[k - 1, :, cols],
+                    g2recv.at[k - 1, :, cols],
+                    7,
+                    c_me,
+                    2 * x + core,
+                    r2sem.at[n],
+                ).start()
+
+    @pl.loop(0, tiles)
     def _(n):
-        at = pl.multiple_of(n * fsize, fsize)
-        for weight, base in ((wg, 0), (wu, FW)):
-            part = jnp.dot(xb[:, :DT], weight[:, pl.ds(at, fsize)], preferred_element_type=f32)
-            gu[:, :, pl.ds(pl.multiple_of(base + at, 128), fsize)] = part.reshape(T, share, fsize).astype(bf16)
-
-    @pl.loop(0, X)
-    def _(x):
-        remote(gu.at[2 * x + 1 - core], g1recv.at[x], 6, c_me, 2 * x_me + 1 - core).start()
-
-    bytes_wait(g1recv, rsem.at[6])
-    tiles = 2 * FW // fsize
-    for k in range(1, X):
-        x = lax.rem(x_me + k, X)
-
-        @pl.loop(0, tiles)
-        def _(n):
-            cols = pl.ds(pl.multiple_of(n * fsize, fsize), fsize)
-            g2send[k - 1, :, cols] = (
-                gu[2 * x + core, :, cols].astype(f32) + g1recv[x, :, cols].astype(f32)
-            ).astype(bf16)
-
-        remote(g2send.at[k - 1], g2recv.at[k - 1], 7, c_me, 2 * x + core).start()
-    if X > 1:
-        bytes_wait(g2recv, rsem.at[7])
+        compute(n)
+
+        @pl.when(n >= 1)
+        def _():
+            across(n - 1)
+
+    across(tiles - 1)
 
     def unit(cols):
         total = gu[t_me, :, cols].astype(f32) + g1recv[x_me, :, cols].astype(f32)
@@ -286,59 +342,94 @@
             total += g2recv[k - 1, :, cols].astype(f32)
         return total
 
-    @pl.loop(0, FW // fsize)
+    def finish(n):
+        if X > 1:
+            bytes_wait(g2recv.at[:, :, pl.ds(0, 2 * fsize)], r2sem.at[n])
+        cols, upper = spans(n)
+        gate = unit(cols)
+        up = unit(upper)
+        hid[t_me, :, cols] = (gate / (1.0 + jnp.exp(-gate)) * up).astype(bf16)
+        own = hid.at[t_me, :, cols]
+        for k in range(1, X):
+            x = lax.rem(x_me + k, X)
+            remote(own, own, 8, c_me, 2 * x + core, r8sem.at[n]).start()
+        remote(own, own, 9, c_me, partner).start()
+
+    def forward(n):
+        if X > 1:
+            cols = spans(n)[0]
+            bytes_wait(hid.at[pl.ds(0, X - 1), :, cols], r8sem.at[n])
+            for k in range(1, X):
+                came = hid.at[2 * lax.rem(x_me + k, X) + core, :, cols]
+                remote(came, came, 9, c_me, partner).start()
+
+    @pl.loop(0, tiles)
     def _(n):
-        at = pl.multiple_of(n * fsize, fsize)
-        gate = unit(pl.ds(at, fsize))
-        up = unit(pl.ds(pl.multiple_of(FW + at, 128), fsize))
-        hid[t_me, :, pl.ds(at, fsize)] = (gate / (1.0 + jnp.exp(-gate)) * up).astype(bf16)
-
-    partner = 2 * x_me + 1 - core
-    for k in range(1, X):
-        remote(hid.at[t_me], hid.at[t_me], 8, c_me, 2 * lax.rem(x_me + k, X) + core).start()
-    remote(hid.at[t_me], hid.at[t_me], 9, c_me, partner).start()
-    if X > 1:
-        bytes_wait(hid.at[pl.ds(0, X - 1)], rsem.at[8])
-        for k in range(1, X):
-            t = 2 * lax.rem(x_me + k, X) + core
-            remote(hid.at[t], hid.at[t], 9, c_me, partner).start()
+        finish(n)
+
+        @pl.when(n >= 2)
+        def _():
+            forward(n - 2)
+
+    for n in range(max(tiles - 2, 0), tiles):
+        forward(n)
     loads[6].wait()
     bytes_wait(hid.at[pl.ds(0, X)], rsem.at[9])
 
     DW = wd.shape[1]
     dsize = tile_of(DW, 256)
 
-    @pl.loop(0, DW // dsize)
-    def _(n):
-        at = pl.multiple_of(n * dsize, dsize)
-        stage[:, pl.ds(at, dsize)] = jnp.dot(
-            hid[...].reshape(N, FW), wd[:, pl.ds(at, dsize)], preferred_element_type=f32
-        )
-
-    for g in range(G):
-        dsend[g] = stage[g * R : (g + 1) * R, :DW].astype(bf16)
-    own = to_all(lambda c, t, g: dsend.at[g], drecv, 10)
-    own.wait()
-    bytes_wait(drecv.at[pl.ds(0, G - 1)], rsem.at[10])
+    parts = dsend.shape[0]
+    span = DW // parts
+    owns = []
+    for p in range(parts):
+
+        @pl.loop(0, span // dsize)
+        def _(n):
+            at = pl.multiple_of(n * dsize, 128)
+            stage[:, pl.ds(at, dsize)] = jnp.dot(
+                hid[...].reshape(N, FW),
+                wd[:, pl.ds(pl.multiple_of(p * span + at, 128), dsize)],
+                preferred_element_type=f32,
+            )
+
+        for g in range(G):
+            dsend[p, g] = stage[g * R : (g + 1) * R, :span].astype(bf16)
+        own = pltpu.make_async_copy(dsend.at[p, g_me], drecv.at[p, g_me], lsem.at[9 + p])
+        own.start()
+        owns.append(own)
+
+        @pl.loop(1, G)
+        def _(k):
+            g = lax.rem(g_me + k, G)
+            remote(
+                dsend.at[p, g], drecv.at[p, g_me], 10, lax.div(g, T), lax.rem(g, T)
+            ).start()
+
+    for own in owns:
+        own.wait()
+    bytes_wait(drecv.at[:, pl.ds(0, G - 1)], rsem.at[10])
     for t in range(T):
-        add = drecv[t].astype(f32)
-        for c in range(1, C):
-            add += drecv[c * T + t].astype(f32)
-        cols = slice(t * DW, (t + 1) * DW)
-        mixed_ref[:, cols] = (attended_ref[:, cols].astype(f32) + add).astype(bf16)
+        for p in range(parts):
+            add = drecv[p, t].astype(f32)
+            for c in range(1, C):
+                add += drecv[p, c * T + t].astype(f32)
+            cols = slice(t * DW + p * span, t * DW + (p + 1) * span)
+            mixed_ref[:, cols] = (attended_ref[:, cols].astype(f32) + add).astype(bf16)
 
     bytes_wait(xrecv.at[pl.ds(0, G - 1)], ssem.at[0])
     bytes_wait(precv.at[pl.ds(0, C - 1)], ssem.at[1])
     bytes_wait(kvbuf.at[pl.ds(0, C - 1)], ssem.at[2])
     bytes_wait(abuf.at[pl.ds(0, C - 1)], ssem.at[3])
     bytes_wait(orecv.at[pl.ds(0, G - 1)], ssem.at[4])
-    bytes_wait(nrecv.at[pl.ds(0, G - 1)], ssem.at[5])
+    bytes_wait(nrecv.at[0, pl.ds(0, T - 1)], ssem.at[5])
+    bytes_wait(nrecv.at[pl.ds(0, C - 1)], ssem.at[11])
     bytes_wait(g1recv, ssem.at[6])
     if X > 1:
         bytes_wait(g2recv, ssem.at[7])
         bytes_wait(hid.at[pl.ds(0, X - 1)], ssem.at[8])
     bytes_wait(hid.at[pl.ds(0, X)], ssem.at[9])
-    bytes_wait(drecv.at[pl.ds(0, G - 1)], ssem.at[10])
+    bytes_wait(drecv.at[:, pl.ds(0, G - 1)], ssem.at[10])
 
 
 def tables(count):
@@ -362,6 +453,8 @@
     vm = pl.BlockSpec(memory_space=pltpu.VMEM)
     hbm = pl.BlockSpec(memory_space=pl.ANY)
     wide = max(DC, DT, OC, DW)
+    tiles = FW // tile_of(FW)
+    parts = 2 if DW % 512 == 0 else 1
 
     def buf(*shape, dtype=bf16):
         return pltpu.VMEM(shape, dtype)
@@ -385,18 +478,23 @@
             buf(G, R, OC),
             buf(G, R, OC),
             buf(T, R, DT),
-            buf(G, R, DT),
+            buf(C, T, R, DT),
             buf(T, N // T, 2 * FW),
             buf(X, N // T, 2 * FW),
             buf(max(X - 1, 1), N // T, 2 * FW),
             buf(max(X - 1, 1), N // T, 2 * FW),
             buf(T, N // T, FW),
-            buf(G, R, DW),
-            buf(G, R, DW),
+            buf(parts, G, R, DW // parts),
+            buf(parts, G, R, DW // parts),
             pltpu.SemaphoreType.DMA((7,)),
-            pltpu.SemaphoreType.DMA((11,)),
-            pltpu.SemaphoreType.DMA((11,)),
-            pltpu.SemaphoreType.DMA((11,)),
+            pltpu.SemaphoreType.DMA((12,)),
+            pltpu.SemaphoreType.DMA((12,)),
+            pltpu.SemaphoreType.DMA((12,)),
+            pltpu.SemaphoreType.DMA((max(C // 2, 1),)),
+            pltpu.SemaphoreType.DMA((max(C // 2, 1),)),
+            pltpu.SemaphoreType.DMA((tiles,)),
+            pltpu.SemaphoreType.DMA((tiles,)),
+            pltpu.SemaphoreType.DMA((tiles,)),
         ],
         compiler_params=pltpu.CompilerParams(
             collective_id=0, has_side_effects=True, vmem_limit_bytes=67043328

time: 123 us -> 111 us (0.902)
  the two profiles are of different devices: /device:TPU:21 before, /device:TPU:0 now
where the time goes in v2:
time: 111 us
  Pallas kernels  107 us (96%)
  local copies, waits for them, and re-layouts  2.98 us (3%)
    pallas_call x1, Pallas kernels, per_device(): pl.pallas_call(functools.partial(kernel, T, C), out_shape=(jax.ShapeDtype...  107 us
    unnamed x2, local copies, waits for them, and re-layouts  2.98 us

profile of v2, /device:TPU:0, one launch (start us, length us, event | category | flops | bytes accessed | tf_op | source)
XLA Modules:
  0.0 110.7 jit_solution(11154617265663179011)
XLA Ops:
  0.6 107.1 %shard_map.131 = (bf16[4,8192]{1,0:T(4,128)(2,1)}, bf16[4,8192]{1,0:T(4,128)(2,1)}) custom-call(bf16[4,8192]{1,0:T(4,128)(2,1)} %tokens.1, f32[1,8192]{1,0:T(1,128)} %bitcast.2, f32[1,8192]{1,0:T(1,128)} %bitcast.3, f32[128,128]{1,0:T(8,128)} %constant.4.clone.cosine, f32[128,128]{1,0:T(8,128)} %constant.5.clone.sine, bf16[1024,2048]{1,0:T(8,128)(2,1)} %wq_h.1, ...), custom_call_target="tpu_custom_call" | custom-call | flops 6845104128 | bytes 53477376 | tf_op jit(solution)/shard_map/pallas_call | solution.py:463
  107.7 1.5 %copy.16 = bf16[4,8192]{1,0:T(4,128)(2,1)} copy(bf16[4,8192]{1,0:T(4,128)(2,1)} %get-tuple-element.4) | data formatting | bytes 131072
  109.2 1.5 %copy.17 = bf16[4,8192]{1,0:T(4,128)(2,1)} copy(bf16[4,8192]{1,0:T(4,128)(2,1)} %get-tuple-element.5) | data formatting | bytes 131072
